TPU v7x, 32 devices: a whole 2x2x4 slice. The times are simulated.
32 devices in a mesh: grid: 8 (over z, y), band: 4 (over x, core).
Axes of the slice: x: 2, y: 2, z: 4, core: 2. Of those that a mesh axis runs over, the one named last changes fastest.
Arguments:
- orbitals: float32 [32, 16, 16, 512], P('grid', None, None, 'band'), may hold values from -80 to 80
- projectors: float32 [32, 16, 16, 512], P('grid', None, None, 'band'), may hold values from -0.09375 to 0.09375
- potential: float32 [32, 16, 16], P('grid'), may hold values from 0.3 to 3
Outputs:
- updated_orbitals: float32 [32, 16, 16, 512], P('grid', None, None, 'band')
- rayleigh_quotients: float32 [3, 512], P(None, 'band')
- residual_norms: float32 [3, 512], P(None, 'band')
All inputs are finite; a program needn't handle non-finite values.
Results may differ from a plain program's by a relative error of at most 0.00012.
Values sent between devices are 32-bit elements; how exact they have to be, the bound alone decides.
A program may use at most 128 MiB of HBM per device.

v0:
```python
import jax
import jax.numpy as jnp
from jax import lax
from jax.sharding import PartitionSpec as P

ITERS = 3
STENCIL = (-205.0 / 72.0, 8.0 / 5.0, -1.0 / 5.0, 8.0 / 315.0, -1.0 / 560.0)
STEP_LENGTH = 0.25
NORM_EPS = 1e-06
HIGHEST = lax.Precision.HIGHEST


def with_halo(block, sides, width):
    for axis, dim in sides:
        count = lax.axis_size(axis)
        forward = [(i, i + 1) for i in range(count - 1)]
        forward.append((count - 1, 0))
        backward = [(target, source) for source, target in forward]
        low = lax.ppermute(
            lax.slice_in_dim(block, block.shape[dim] - width, None, axis=dim), axis, forward
        )
        high = lax.ppermute(lax.slice_in_dim(block, 0, width, axis=dim), axis, backward)
        block = jnp.concatenate([low, block, high], axis=dim)
    return block


def matmul(left, right):
    return jnp.dot(left, right, precision=HIGHEST, preferred_element_type=jnp.float32)


def laplacian(grid_field):
    padded = with_halo(grid_field, (("grid", 0),), 4)
    planes_here = grid_field.shape[0]
    result = 3.0 * STENCIL[0] * grid_field
    for distance in range(1, 5):
        result = result + STENCIL[distance] * (
            padded[4 + distance : 4 + distance + planes_here]
            + padded[4 - distance : 4 - distance + planes_here]
        )
    for dimension in (1, 2):
        for distance in range(1, 5):
            result = result + STENCIL[distance] * (
                jnp.roll(grid_field, distance, dimension)
                + jnp.roll(grid_field, -distance, dimension)
            )
    return result


def local(orbitals, projectors, potential):
    grid_shape = orbitals.shape
    local_bands = orbitals.shape[3]
    total_bands = local_bands * lax.axis_size("band")
    first_band = lax.axis_index("band") * local_bands
    vectors = orbitals.reshape(-1, local_bands)
    every_projector = lax.all_gather(projectors, "band", axis=3, tiled=True).reshape(
        -1, projectors.shape[3] * lax.axis_size("band")
    )
    identity_matrix = jnp.eye(total_bands, dtype=jnp.float32)
    quotient_list = []
    norm_list = []
    for iteration in range(ITERS):
        gathered = lax.all_gather(vectors.reshape(grid_shape), "band", axis=3, tiled=True).reshape(
            -1, total_bands
        )
        margin = lax.psum(matmul(gathered.T, gathered), "grid")
        factor = jnp.linalg.cholesky(margin)
        inverse = jax.scipy.linalg.solve_triangular(factor, identity_matrix, lower=True)
        transform = inverse.T
        vectors = matmul(gathered, lax.dynamic_slice_in_dim(transform, first_band, local_bands, 1))
        coupling = lax.psum(matmul(every_projector.T, vectors), "grid")
        exchange_part = matmul(every_projector, coupling)
        grid_field = vectors.reshape(grid_shape)
        applied = (-0.5 * laplacian(grid_field) + potential[..., None] * grid_field).reshape(
            -1, local_bands
        ) - exchange_part
        rayleigh = lax.psum(jnp.sum(vectors * applied, axis=0), "grid")
        residual = applied - rayleigh[None, :] * vectors
        squared = lax.psum(jnp.sum(residual * residual, axis=0), "grid")
        vectors = vectors - STEP_LENGTH * residual / jnp.sqrt(squared + NORM_EPS)[None, :]
        quotient_list.append(rayleigh)
        norm_list.append(jnp.sqrt(squared))
    return (vectors.reshape(grid_shape), jnp.stack(quotient_list), jnp.stack(norm_list))


def solution(mesh):
    return jax.shard_map(
        local,
        mesh=mesh,
        in_specs=(
            P("grid", None, None, "band"),
            P("grid", None, None, "band"),
            P("grid", None, None),
        ),
        out_specs=(P("grid", None, None, "band"), P(None, "band"), P(None, "band")),
        check_vma=False,
    )
```

profile of v0, /device:TPU:0, one launch (start us, length us, event | category | flops | bytes accessed | tf_op | source)
XLA Modules:
  0.0 1202.1 jit_solution(3516485684897773808)
XLA Ops:
  7.9 27.1 %all-gather.5.cloned.1.call-done = f32[4,16,16,512]{3,2,1,0:T(8,128)} async-done(((f32[4,16,16,128]{3,2,1,0:T(8,128)}), f32[4,16,16,512]{3,2,1,0:T(8,128)}) %all-gather.5.cloned.1.call-update) | async-done | bytes 2097168 | tf_op jit(solution)/shard_map/all_gather | solution.py:62
  43.0 77.3 %all-reduce.8.cloned.1.call-done = f32[512,512]{0,1:T(8,128)} async-done(((f32[512,512]{0,1:T(8,128)}), f32[512,512]{0,1:T(8,128)}) %all-reduce.8.cloned.1.call-update) | async-done | bytes 1048592 | tf_op jit(solution)/shard_map/psum | solution.py:65
  123.2 11.7 cholesky.374
  147.4 11.7 cholesky.393
  171.0 11.7 cholesky.414
  194.7 11.7 cholesky.431
  218.7 39.3 %custom-call.34 = f32[4,128,128]{1,2,0:T(8,128)S(1)} custom-call(f32[4,128,128]{2,1,0:T(8,128)S(1)} %get-tuple-element.25), custom_call_target="InvertDiagBlocksLowerTriangular" | custom-call | tf_op jit(solution)/shard_map/jit(_solve_triangular)/triangular_solve | solution.py:67
  296.4 58.0 %all-reduce.10.cloned.1.call-done = f32[512,128]{0,1:T(8,128)} async-done(((f32[512,128]{0,1:T(8,128)}), f32[512,128]{0,1:T(8,128)}) %all-reduce.10.cloned.1.call-update) | async-done | bytes 262160 | tf_op jit(solution)/shard_map/psum | solution.py:70
  357.9 19.6 %psum.86 = f32[128]{0:T(128)S(1)} all-reduce(f32[128]{0:T(128)S(1)} %get-tuple-element.195), channel_id=1, replica_groups=mesh['grid'=8,'band'=4] {'grid'}, use_global_device_ids=true, to_apply=%region_11.14 | all-reduce | flops 128 | bytes 1024 | tf_op jit(solution)/shard_map/psum | solution.py:76
  377.8 17.1 %psum.87 = f32[128]{0:T(128)S(1)} all-reduce(f32[128]{0:T(128)S(1)} %multiply_reduce_fusion.4), channel_id=1, replica_groups=mesh['grid'=8,'band'=4] {'grid'}, use_global_device_ids=true, to_apply=%region_13.16 | all-reduce | flops 128 | bytes 1024 | tf_op jit(solution)/shard_map/psum | solution.py:78
  398.0 21.6 %all-gather.9.cloned.1.call-done = f32[4,16,16,512]{3,2,1,0:T(8,128)} async-done(((f32[4,16,16,128]{3,2,1,0:T(8,128)}), f32[4,16,16,512]{3,2,1,0:T(8,128)}) %all-gather.9.cloned.1.call-update) | async-done | bytes 2097168 | tf_op jit(solution)/shard_map/all_gather | solution.py:62
  426.8 77.9 %all-reduce.12.cloned.1.call-done = f32[512,512]{0,1:T(8,128)} async-done(((f32[512,512]{0,1:T(8,128)}), f32[512,512]{0,1:T(8,128)}) %all-reduce.12.cloned.1.call-update) | async-done | bytes 1048592 | tf_op jit(solution)/shard_map/psum | solution.py:65
  509.8 11.7 cholesky.446
  534.0 11.7 cholesky.465
  559.6 11.7 cholesky.486
  584.6 11.7 cholesky.503
  602.6 11.8 while.7
  615.1 40.1 %custom-call.38 = f32[4,128,128]{1,2,0:T(8,128)S(1)} custom-call(f32[4,128,128]{2,1,0:T(8,128)} %copy-done.45), custom_call_target="InvertDiagBlocksLowerTriangular" | custom-call | tf_op jit(solution)/shard_map/jit(_solve_triangular)/triangular_solve | solution.py:67
  680.7 14.4 %collective-permute-done.2 = f32[4,16,16,128]{3,2,1,0:T(8,128)} collective-permute-done((f32[4,16,16,128]{3,2,1,0:T(8,128)S(1)}, f32[4,16,16,128]{3,2,1,0:T(8,128)}, u32[]{:S(2)}, u32[]{:S(2)}) %collective-permute-start.2) | collective-permute-done | bytes 524320 | tf_op jit(solution)/shard_map/ppermute | solution.py:22
  701.9 51.0 %all-reduce.14.cloned.1.call-done = f32[512,128]{0,1:T(8,128)} async-done(((f32[512,128]{0,1:T(8,128)}), f32[512,128]{0,1:T(8,128)}) %all-reduce.14.cloned.1.call-update) | async-done | bytes 262160 | tf_op jit(solution)/shard_map/psum | solution.py:70
  756.4 19.6 %psum.90 = f32[128]{0:T(128)S(1)} all-reduce(f32[128]{0:T(128)S(1)} %get-tuple-element.199), channel_id=1, replica_groups=mesh['grid'=8,'band'=4] {'grid'}, use_global_device_ids=true, to_apply=%region_17.20 | all-reduce | flops 128 | bytes 1024 | tf_op jit(solution)/shard_map/psum | solution.py:76
  776.2 17.1 %psum.91 = f32[128]{0:T(128)S(1)} all-reduce(f32[128]{0:T(128)S(1)} %multiply_reduce_fusion.2), channel_id=1, replica_groups=mesh['grid'=8,'band'=4] {'grid'}, use_global_device_ids=true, to_apply=%region_19.22 | all-reduce | flops 128 | bytes 1024 | tf_op jit(solution)/shard_map/psum | solution.py:78
  797.0 21.6 %all-gather.11.cloned.1.call-done = f32[4,16,16,512]{3,2,1,0:T(8,128)} async-done(((f32[4,16,16,128]{3,2,1,0:T(8,128)}), f32[4,16,16,512]{3,2,1,0:T(8,128)}) %all-gather.11.cloned.1.call-update) | async-done | bytes 2097168 | tf_op jit(solution)/shard_map/all_gather | solution.py:62
  825.5 78.3 %all-reduce.16.cloned.1.call-done = f32[512,512]{0,1:T(8,128)} async-done(((f32[512,512]{0,1:T(8,128)}), f32[512,512]{0,1:T(8,128)}) %all-reduce.16.cloned.1.call-update) | async-done | bytes 1048592 | tf_op jit(solution)/shard_map/psum | solution.py:65
  908.8 11.7 cholesky.518
  983.7 11.7 cholesky.575
  1001.9 11.8 while.8
  1014.4 40.1 %custom-call.42 = f32[4,128,128]{1,2,0:T(8,128)S(1)} custom-call(f32[4,128,128]{2,1,0:T(8,128)} %copy-done.44), custom_call_target="InvertDiagBlocksLowerTriangular" | custom-call | tf_op jit(solution)/shard_map/jit(_solve_triangular)/triangular_solve | solution.py:67
  1079.6 14.8 %collective-permute-done.4 = f32[4,16,16,128]{3,2,1,0:T(8,128)} collective-permute-done((f32[4,16,16,128]{3,2,1,0:T(8,128)S(1)}, f32[4,16,16,128]{3,2,1,0:T(8,128)}, u32[]{:S(2)}, u32[]{:S(2)}) %collective-permute-start.4) | collective-permute-done | bytes 524320 | tf_op jit(solution)/shard_map/ppermute | solution.py:22
  1101.2 51.0 %all-reduce.18.cloned.1.call-done = f32[512,128]{0,1:T(8,128)} async-done(((f32[512,128]{0,1:T(8,128)}), f32[512,128]{0,1:T(8,128)}) %all-reduce.18.cloned.1.call-update) | async-done | bytes 262160 | tf_op jit(solution)/shard_map/psum | solution.py:70
  1155.7 19.6 %psum.94 = f32[128]{0:T(128)S(1)} all-reduce(f32[128]{0:T(128)S(1)} %get-tuple-element.203), channel_id=1, replica_groups=mesh['grid'=8,'band'=4] {'grid'}, use_global_device_ids=true, to_apply=%region_23.26 | all-reduce | flops 128 | bytes 1024 | tf_op jit(solution)/shard_map/psum | solution.py:76
  1175.5 17.1 %psum.95 = f32[128]{0:T(128)S(1)} all-reduce(f32[128]{0:T(128)S(1)} %multiply_reduce_fusion), channel_id=1, replica_groups=mesh['grid'=8,'band'=4] {'grid'}, use_global_device_ids=true, to_apply=%region_25.28 | all-reduce | flops 128 | bytes 1024 | tf_op jit(solution)/shard_map/psum | solution.py:78
  (345 shorter events, 347.1 us)
Async XLA Ops:
  7.2 27.9 %all-gather.5.cloned.1.call-start = ((), (), s32[]{:S(2)}) async-start(), calls=%async_computation | async-start | bytes 2621440 | tf_op jit(solution)/shard_map/all_gather | solution.py:62
  7.9 112.4 %all-reduce.8.cloned.1.call-start = ((), (), s32[]{:S(2)}) async-start(), calls=%async_computation.1 | async-start | bytes 2097152 | tf_op jit(solution)/shard_map/psum | solution.py:65
  41.8 236.4 %all-gather.7.cloned.1.call-start = ((), (), s32[]{:S(2)}) async-start(), calls=%async_computation.2 | async-start | bytes 2621440 | tf_op jit(solution)/shard_map/all_gather | solution.py:55
  42.5 311.9 %all-reduce.10.cloned.1.call-start = ((), (), s32[]{:S(2)}) async-start(), calls=%async_computation.3 | async-start | bytes 524288 | tf_op jit(solution)/shard_map/psum | solution.py:70
  43.0 217.1 %copy-start.4 = (f32[512,512]{1,0:T(8,128)}, f32[512,512]{1,0:T(8,128)S(1)}, u32[]{:S(2)}) copy-start(f32[512,512]{1,0:T(8,128)S(1)} %fusion.6) | copy-start | bytes 3145732
  263.7 24.9 %collective-permute-start = (f32[4,16,16,128]{3,2,1,0:T(8,128)S(1)}, f32[4,16,16,128]{3,2,1,0:T(8,128)S(1)}, u32[]{:S(2)}, u32[]{:S(2)}) collective-permute-start(f32[4,16,16,128]{3,2,1,0:T(8,128)S(1)} %bitcast.253), channel_id=1, source_target_pairs={{4,0},{8,4},{12,8},{16,12},{20,16},{24,20},{28,24},{0,28},{5,1},{9... | collective-permute-start | bytes 1572872 | tf_op jit(solution)/shard_map/ppermute | solution.py:22
  266.7 21.9 %collective-permute-start.1 = (f32[4,16,16,128]{3,2,1,0:T(8,128)S(1)}, f32[4,16,16,128]{3,2,1,0:T(8,128)S(1)}, u32[]{:S(2)}, u32[]{:S(2)}) collective-permute-start(f32[4,16,16,128]{3,2,1,0:T(8,128)S(1)} %bitcast.254), channel_id=1, source_target_pairs={{0,4},{4,8},{8,12},{12,16},{16,20},{20,24},{24,28},{28,0},{1,5},{5... | collective-permute-start | bytes 1572872 | tf_op jit(solution)/shard_map/ppermute | solution.py:19
  281.8 137.8 %all-gather.9.cloned.1.call-start = ((), (), s32[]{:S(2)}) async-start(), calls=%async_computation.4 | async-start | bytes 2621440 | tf_op jit(solution)/shard_map/all_gather | solution.py:62
  289.6 64.8 %copy-start = (f32[4,16,16,512]{3,2,1,0:T(8,128)S(1)}, f32[4,16,16,512]{3,2,1,0:T(8,128)}, u32[]{:S(2)}) copy-start(f32[4,16,16,512]{3,2,1,0:T(8,128)} %all-gather.7.cloned.1.call-done) | copy-start | bytes 6291460
  398.0 106.8 %all-reduce.12.cloned.1.call-start = ((), (), s32[]{:S(2)}) async-start(), calls=%async_computation.5 | async-start | bytes 2097152 | tf_op jit(solution)/shard_map/psum | solution.py:65
  426.3 326.6 %all-reduce.14.cloned.1.call-start = ((), (), s32[]{:S(2)}) async-start(), calls=%async_computation.6 | async-start | bytes 524288 | tf_op jit(solution)/shard_map/psum | solution.py:70
  559.6 95.7 %copy-start.5 = (f32[512,512]{1,0:T(8,128)S(1)}, f32[512,512]{1,0:T(8,128)}, u32[]{:S(2)}) copy-start(f32[512,512]{1,0:T(8,128)} %copy-done.4) | copy-start | bytes 3145732
  669.1 26.0 %collective-permute-start.2 = (f32[4,16,16,128]{3,2,1,0:T(8,128)S(1)}, f32[4,16,16,128]{3,2,1,0:T(8,128)}, u32[]{:S(2)}, u32[]{:S(2)}) collective-permute-start(f32[4,16,16,128]{3,2,1,0:T(8,128)S(1)} %bitcast.221), channel_id=1, source_target_pairs={{4,0},{8,4},{12,8},{16,12},{20,16},{24,20},{28,24},{0,28},{5,1},{9... | collective-permute-start | bytes 1572872 | tf_op jit(solution)/shard_map/ppermute | solution.py:22
  672.0 23.1 %collective-permute-start.3 = (f32[4,16,16,128]{3,2,1,0:T(8,128)S(1)}, f32[4,16,16,128]{3,2,1,0:T(8,128)}, u32[]{:S(2)}, u32[]{:S(2)}) collective-permute-start(f32[4,16,16,128]{3,2,1,0:T(8,128)S(1)} %bitcast.222), channel_id=1, source_target_pairs={{0,4},{4,8},{8,12},{12,16},{16,20},{20,24},{24,28},{28,0},{1,5},{5... | collective-permute-start | bytes 1572872 | tf_op jit(solution)/shard_map/ppermute | solution.py:19
  680.0 138.6 %all-gather.11.cloned.1.call-start = ((), (), s32[]{:S(2)}) async-start(), calls=%async_computation.7 | async-start | bytes 2621440 | tf_op jit(solution)/shard_map/all_gather | solution.py:62
  680.4 14.7 %copy-start.15 = (f32[4,16,15,128]{3,2,1,0:T(8,128)S(1)}, f32[4,16,15,128]{3,2,1,0:T(8,128)}, u32[]{:S(2)}) copy-start(f32[4,16,15,128]{3,2,1,0:T(8,128)} %get-tuple-element.111) | copy-start | bytes 1474564
  680.5 14.7 %copy-start.16 = (f32[4,16,15,128]{3,2,1,0:T(8,128)S(1)}, f32[4,16,15,128]{3,2,1,0:T(8,128)}, u32[]{:S(2)}) copy-start(f32[4,16,15,128]{3,2,1,0:T(8,128)} %get-tuple-element.112) | copy-start | bytes 1474564
  796.9 106.8 %all-reduce.16.cloned.1.call-start = ((), (), s32[]{:S(2)}) async-start(), calls=%async_computation.8 | async-start | bytes 2097152 | tf_op jit(solution)/shard_map/psum | solution.py:65
  825.3 326.9 %all-reduce.18.cloned.1.call-start = ((), (), s32[]{:S(2)}) async-start(), calls=%async_computation.9 | async-start | bytes 524288 | tf_op jit(solution)/shard_map/psum | solution.py:70
  958.7 95.8 %copy-start.6 = (f32[512,512]{1,0:T(8,128)S(1)}, f32[512,512]{1,0:T(8,128)}, u32[]{:S(2)}) copy-start(f32[512,512]{1,0:T(8,128)} %copy-done.4) | copy-start | bytes 3145732
  1068.4 26.0 %collective-permute-start.4 = (f32[4,16,16,128]{3,2,1,0:T(8,128)S(1)}, f32[4,16,16,128]{3,2,1,0:T(8,128)}, u32[]{:S(2)}, u32[]{:S(2)}) collective-permute-start(f32[4,16,16,128]{3,2,1,0:T(8,128)S(1)} %bitcast.240), channel_id=1, source_target_pairs={{4,0},{8,4},{12,8},{16,12},{20,16},{24,20},{28,24},{0,28},{5,1},{9... | collective-permute-start | bytes 1572872 | tf_op jit(solution)/shard_map/ppermute | solution.py:22
  1071.3 23.1 %collective-permute-start.5 = (f32[4,16,16,128]{3,2,1,0:T(8,128)S(1)}, f32[4,16,16,128]{3,2,1,0:T(8,128)}, u32[]{:S(2)}, u32[]{:S(2)}) collective-permute-start(f32[4,16,16,128]{3,2,1,0:T(8,128)S(1)} %bitcast.241), channel_id=1, source_target_pairs={{0,4},{4,8},{8,12},{12,16},{16,20},{20,24},{24,28},{28,0},{1,5},{5... | collective-permute-start | bytes 1572872 | tf_op jit(solution)/shard_map/ppermute | solution.py:19
  1079.4 15.0 %copy-start.21 = (f32[4,16,15,128]{3,2,1,0:T(8,128)S(1)}, f32[4,16,15,128]{3,2,1,0:T(8,128)}, u32[]{:S(2)}) copy-start(f32[4,16,15,128]{3,2,1,0:T(8,128)} %get-tuple-element.79) | copy-start | bytes 1474564
  1079.4 15.0 %copy-start.22 = (f32[4,16,15,128]{3,2,1,0:T(8,128)S(1)}, f32[4,16,15,128]{3,2,1,0:T(8,128)}, u32[]{:S(2)}) copy-start(f32[4,16,15,128]{3,2,1,0:T(8,128)} %get-tuple-element.80) | copy-start | bytes 1474564
  1079.4 15.0 %copy-start.23 = (f32[4,16,14,128]{3,2,1,0:T(8,128)S(1)}, f32[4,16,14,128]{3,2,1,0:T(8,128)}, u32[]{:S(2)}) copy-start(f32[4,16,14,128]{3,2,1,0:T(8,128)} %get-tuple-element.83) | copy-start | bytes 1376260
  1079.4 15.0 %copy-start.24 = (f32[4,16,14,128]{3,2,1,0:T(8,128)S(1)}, f32[4,16,14,128]{3,2,1,0:T(8,128)}, u32[]{:S(2)}) copy-start(f32[4,16,14,128]{3,2,1,0:T(8,128)} %get-tuple-element.84) | copy-start | bytes 1376260
  1079.4 15.0 %copy-start.25 = (f32[4,16,13,128]{3,2,1,0:T(8,128)S(1)}, f32[4,16,13,128]{3,2,1,0:T(8,128)}, u32[]{:S(2)}) copy-start(f32[4,16,13,128]{3,2,1,0:T(8,128)} %get-tuple-element.87) | copy-start | bytes 1277956
  1079.4 15.0 %copy-start.26 = (f32[4,16,13,128]{3,2,1,0:T(8,128)S(1)}, f32[4,16,13,128]{3,2,1,0:T(8,128)}, u32[]{:S(2)}) copy-start(f32[4,16,13,128]{3,2,1,0:T(8,128)} %get-tuple-element.88) | copy-start | bytes 1277956
  1079.4 15.0 %copy-start.35 = (f32[4,14,16,128]{3,2,1,0:T(8,128)S(1)}, f32[4,14,16,128]{3,2,1,0:T(8,128)}, u32[]{:S(2)}) copy-start(f32[4,14,16,128]{3,2,1,0:T(8,128)} %get-tuple-element.67) | copy-start | bytes 1376260
  1079.4 15.0 %copy-start.36 = (f32[4,14,16,128]{3,2,1,0:T(8,128)S(1)}, f32[4,14,16,128]{3,2,1,0:T(8,128)}, u32[]{:S(2)}) copy-start(f32[4,14,16,128]{3,2,1,0:T(8,128)} %get-tuple-element.68) | copy-start | bytes 1376260
  1079.5 15.0 %copy-start.43 = (f32[4,16,16]{2,1,0:T(8,128)S(1)}, f32[4,16,16]{2,1,0:T(8,128)}, u32[]{:S(2)}) copy-start(f32[4,16,16]{2,1,0:T(8,128)} %param.8) | copy-start | bytes 12292
  1155.7 38.2 %copy-start.46 = (f32[1,128]{1,0:T(1,128)S(1)}, f32[1,128]{1,0:T(1,128)}, u32[]{:S(2)}) copy-start(f32[1,128]{1,0:T(1,128)} %get-tuple-element.189) | copy-start | bytes 1540
  (31 other events, 195.8 us)
Sparse Core Ops, SparseCore 0:
  9.5 25.5 all-gather.4
  41.9 78.3 all-reduce.7
  121.8 22.4 all-gather.6
  282.0 72.4 all-reduce.9
  398.1 21.4 all-gather.8
  426.4 78.2 all-reduce.11
  680.1 72.7 all-reduce.13
  797.0 21.4 all-gather.10
  825.4 78.3 all-reduce.15
  1079.5 72.6 all-reduce.17
where the time goes:
time: 1210 us; the launch traced here: 1200 us
  waiting for transfers between devices  501 us (41%)
  other arithmetic  387 us (32%)
  blocking collectives  110 us (9%)
  local copies, waits for them, and re-layouts  93.1 us (8%)
  matrix products  77.4 us (6%)
  between operations  22.9 us (2%)
    another operation x44, other arithmetic, local(): factor = jnp.linalg.cholesky(margin)  240 us
    psum x3, waiting for transfers between devices, local(): margin = lax.psum(matmul(gathered.T, gathered), 'grid')  233 us
    psum x3, waiting for transfers between devices, local(): coupling = lax.psum(matmul(every_projector.T, vectors), 'grid')  160 us
    another operation x7, other arithmetic, local(): jax.scipy.linalg.solve_triangular(factor, identity_matrix, lower=True)  125 us
    all_gather x3, waiting for transfers between devices, local(): lax.all_gather(vectors.reshape(grid_shape), 'band', axis=3, tiled=True)  70.3 us
    psum x3, blocking collectives, local(): rayleigh = lax.psum(jnp.sum(vectors * applied, axis=0), 'grid')  58.9 us
    psum x3, blocking collectives, local(): squared = lax.psum(jnp.sum(residual * residual, axis=0), 'grid')  51.4 us
    dot_general x12, matrix products, matmul(): jnp.dot(left, right, precision=HIGHEST, preferred_element_type=jnp.float32)  44.3 us
  transfers between devices with their start and end apart: 16, of which 12 were waited for; matrix products, arithmetic and copies ran while one was open for 16% of the time, Pallas kernels for 0%

commit v1 on v0

--- a/solution.py
+++ b/solution.py
@@ -67,7 +67,7 @@
         inverse = jax.scipy.linalg.solve_triangular(factor, identity_matrix, lower=True)
         transform = inverse.T
         vectors = matmul(gathered, lax.dynamic_slice_in_dim(transform, first_band, local_bands, 1))
-        coupling = lax.psum(matmul(every_projector.T, vectors), "grid")
+        coupling = jnp.sum(lax.all_gather(matmul(every_projector.T, vectors), "grid"), axis=0)
         exchange_part = matmul(every_projector, coupling)
         grid_field = vectors.reshape(grid_shape)
         applied = (-0.5 * laplacian(grid_field) + potential[..., None] * grid_field).reshape(

time: 1210 us -> 1130 us (0.934)
  waiting for transfers between devices: 501 us -> 443 us
  local copies, waits for them, and re-layouts: 93.1 us -> 77.8 us
    psum x3 -> x0, waiting for transfers between devices: 160 us -> none  [local(): coupling = lax.psum(matmul(every_projector.T, vectors), 'grid')]
    all_gather x0 -> x3, waiting for transfers between devices: none -> 77.7 us  [local(): lax.all_gather(matmul(every_projector.T, vectors), 'grid')]
    slice x48, local copies, waits for them, and re-layouts: 35.1 us -> 4.23 us  [laplacian(): jnp.roll(grid_field, distance, dimension)]
    ppermute x3, waiting for transfers between devices: 35.4 us -> 60.6 us  [with_halo(): lax.ppermute(lax.slice_in_dim(block, 0, width, axis=dim), axis, backward)]
  transfers between devices with their start and end apart: 16 -> 16, of which waited for: 12 -> 12; matrix products, arithmetic and copies ran while one was open for 16% -> 15% of each run, Pallas kernels for 0% -> 0%
where the time goes in v1:
time: 1130 us
  waiting for transfers between devices  443 us (39%)
  other arithmetic  387 us (34%)
  blocking collectives  109 us (10%)
  local copies, waits for them, and re-layouts  77.8 us (7%)
  matrix products  77.7 us (7%)
  between operations  23.4 us (2%)
    another operation x44, other arithmetic, local(): factor = jnp.linalg.cholesky(margin)  240 us
    psum x3, waiting for transfers between devices, local(): margin = lax.psum(matmul(gathered.T, gathered), 'grid')  233 us
    another operation x7, other arithmetic, local(): jax.scipy.linalg.solve_triangular(factor, identity_matrix, lower=True)  126 us
    all_gather x3, waiting for transfers between devices, local(): lax.all_gather(matmul(every_projector.T, vectors), 'grid')  77.7 us
    all_gather x3, waiting for transfers between devices, local(): lax.all_gather(vectors.reshape(grid_shape), 'band', axis=3, tiled=True)  70 us
    ppermute x3, waiting for transfers between devices, with_halo(): lax.ppermute(lax.slice_in_dim(block, 0, width, axis=dim), axis, backward)  60.6 us
    psum x3, blocking collectives, local(): rayleigh = lax.psum(jnp.sum(vectors * applied, axis=0), 'grid')  56.9 us
    psum x3, blocking collectives, local(): squared = lax.psum(jnp.sum(residual * residual, axis=0), 'grid')  52 us
  transfers between devices with their start and end apart: 16, of which 12 were waited for; matrix products, arithmetic and copies ran while one was open for 15% of the time, Pallas kernels for 0%

profile of v1, /device:TPU:0, one launch (start us, length us, event | category | flops | bytes accessed | tf_op | source)
XLA Modules:
  0.0 1128.7 jit_solution(13358649261294858395)
XLA Ops:
  7.9 27.1 %all-gather.11.cloned.1.call-done = f32[4,16,16,512]{3,2,1,0:T(8,128)} async-done(((f32[4,16,16,128]{3,2,1,0:T(8,128)}), f32[4,16,16,512]{3,2,1,0:T(8,128)}) %all-gather.11.cloned.1.call-update) | async-done | bytes 2097168 | tf_op jit(solution)/shard_map/all_gather | solution.py:62
  43.2 77.1 %all-reduce.5.cloned.1.call-done = f32[512,512]{0,1:T(8,128)} async-done(((f32[512,512]{0,1:T(8,128)}), f32[512,512]{0,1:T(8,128)}) %all-reduce.5.cloned.1.call-update) | async-done | bytes 1048592 | tf_op jit(solution)/shard_map/psum | solution.py:65
  123.2 11.7 %cholesky.374 = f32[128,128]{1,0:T(8,128)S(1)} custom-call(f32[128,128]{1,0:T(8,128)S(1)} %cholesky.586), custom_call_target="Cholesky" | custom-call | tf_op jit(solution)/shard_map/jit(cholesky)/cholesky | solution.py:66
  147.4 11.7 %cholesky.393 = f32[128,128]{1,0:T(8,128)S(1)} custom-call(f32[128,128]{1,0:T(8,128)S(1)} %cholesky.590), custom_call_target="Cholesky" | custom-call | tf_op jit(solution)/shard_map/jit(cholesky)/cholesky | solution.py:66
  170.7 11.7 %cholesky.414 = f32[128,128]{1,0:T(8,128)S(1)} custom-call(f32[128,128]{1,0:T(8,128)S(1)} %cholesky.595), custom_call_target="Cholesky" | custom-call | tf_op jit(solution)/shard_map/jit(cholesky)/cholesky | solution.py:66
  194.4 11.7 %cholesky.431 = f32[128,128]{1,0:T(8,128)S(1)} custom-call(f32[128,128]{1,0:T(8,128)S(1)} %convolution_subtract_fusion.17), custom_call_target="Cholesky" | custom-call | tf_op jit(solution)/shard_map/jit(cholesky)/cholesky | solution.py:66
  218.7 39.3 %custom-call.34 = f32[4,128,128]{1,2,0:T(8,128)S(1)} custom-call(f32[4,128,128]{2,1,0:T(8,128)S(1)} %get-tuple-element.25), custom_call_target="InvertDiagBlocksLowerTriangular" | custom-call | tf_op jit(solution)/shard_map/jit(_solve_triangular)/triangular_solve | solution.py:67
  272.2 19.1 %collective-permute-done = f32[4,16,16,128]{3,2,1,0:T(8,128)S(1)} collective-permute-done((f32[4,16,16,128]{3,2,1,0:T(8,128)S(1)}, f32[4,16,16,128]{3,2,1,0:T(8,128)S(1)}, u32[]{:S(2)}, u32[]{:S(2)}) %collective-permute-start) | collective-permute-done | bytes 524320 | tf_op jit(solution)/shard_map/ppermute | solution.py:22
  296.4 27.5 %all-gather.19.cloned.1.call-done = f32[4096,128]{0,1:T(8,128)} async-done(((f32[512,128]{0,1:T(8,128)}), f32[4096,128]{0,1:T(8,128)}) %all-gather.19.cloned.1.call-update) | async-done | bytes 2097168 | tf_op jit(solution)/shard_map/all_gather | solution.py:70
  331.2 19.0 %psum.64 = f32[128]{0:T(128)S(1)} all-reduce(f32[128]{0:T(128)S(1)} %get-tuple-element.195), channel_id=1, replica_groups=mesh['grid'=8,'band'=4] {'grid'}, use_global_device_ids=true, to_apply=%region_11.14 | all-reduce | flops 128 | bytes 1024 | tf_op jit(solution)/shard_map/psum | solution.py:76
  350.4 17.3 %psum.65 = f32[128]{0:T(128)S(1)} all-reduce(f32[128]{0:T(128)S(1)} %multiply_reduce_fusion.4), channel_id=1, replica_groups=mesh['grid'=8,'band'=4] {'grid'}, use_global_device_ids=true, to_apply=%region_13.16 | all-reduce | flops 128 | bytes 1024 | tf_op jit(solution)/shard_map/psum | solution.py:78
  370.8 21.4 %all-gather.15.cloned.1.call-done = f32[4,16,16,512]{3,2,1,0:T(8,128)} async-done(((f32[4,16,16,128]{3,2,1,0:T(8,128)}), f32[4,16,16,512]{3,2,1,0:T(8,128)}) %all-gather.15.cloned.1.call-update) | async-done | bytes 2097168 | tf_op jit(solution)/shard_map/all_gather | solution.py:62
  399.2 78.2 %all-reduce.7.cloned.1.call-done = f32[512,512]{0,1:T(8,128)} async-done(((f32[512,512]{0,1:T(8,128)}), f32[512,512]{0,1:T(8,128)}) %all-reduce.7.cloned.1.call-update) | async-done | bytes 1048592 | tf_op jit(solution)/shard_map/psum | solution.py:65
  482.5 11.7 %cholesky.446 = f32[128,128]{1,0:T(8,128)S(1)} custom-call(f32[128,128]{1,0:T(8,128)S(1)} %cholesky.599), custom_call_target="Cholesky" | custom-call | tf_op jit(solution)/shard_map/jit(cholesky)/cholesky | solution.py:66
  506.7 11.7 %cholesky.465 = f32[128,128]{1,0:T(8,128)S(1)} custom-call(f32[128,128]{1,0:T(8,128)S(1)} %cholesky.603), custom_call_target="Cholesky" | custom-call | tf_op jit(solution)/shard_map/jit(cholesky)/cholesky | solution.py:66
  532.4 11.7 %cholesky.486 = f32[128,128]{1,0:T(8,128)S(1)} custom-call(f32[128,128]{1,0:T(8,128)S(1)} %cholesky.608), custom_call_target="Cholesky" | custom-call | tf_op jit(solution)/shard_map/jit(cholesky)/cholesky | solution.py:66
  557.5 11.7 %cholesky.503 = f32[128,128]{1,0:T(8,128)S(1)} custom-call(f32[128,128]{1,0:T(8,128)S(1)} %convolution_subtract_fusion.16), custom_call_target="Cholesky" | custom-call | tf_op jit(solution)/shard_map/jit(cholesky)/cholesky | solution.py:66
  576.6 14.1 %while.7 = (s32[]{:T(128)}, f32[512,512]{1,0:T(8,128)}, s32[4,2]{0,1:T(2,128)S(1)}, f32[4,128,128]{2,1,0:T(8,128)}, s32[]{:T(128)}) while((s32[]{:T(128)}, f32[512,512]{1,0:T(8,128)}, s32[4,2]{0,1:T(2,128)S(1)}, f32[4,128,128]{2,1,0:T(8,128)}, s32[]{:T(128)}) %tuple.160), condition=%wide.while_cond.clone, body=%wide.while_body.clone.sunk | while | flops 2 | bytes 132705 | solution.py:67
  590.8 40.7 %custom-call.38 = f32[4,128,128]{1,2,0:T(8,128)} custom-call(f32[4,128,128]{2,1,0:T(8,128)} %get-tuple-element.26), custom_call_target="InvertDiagBlocksLowerTriangular" | custom-call | tf_op jit(solution)/shard_map/jit(_solve_triangular)/triangular_solve | solution.py:67
  648.3 20.7 %collective-permute-done.2 = f32[4,16,16,128]{3,2,1,0:T(8,128)} collective-permute-done((f32[4,16,16,128]{3,2,1,0:T(8,128)S(1)}, f32[4,16,16,128]{3,2,1,0:T(8,128)}, u32[]{:S(2)}, u32[]{:S(2)}) %collective-permute-start.2) | collective-permute-done | bytes 524320 | tf_op jit(solution)/shard_map/ppermute | solution.py:22
  675.2 25.0 %all-gather.21.cloned.1.call-done = f32[4096,128]{0,1:T(8,128)} async-done(((f32[512,128]{0,1:T(8,128)}), f32[4096,128]{0,1:T(8,128)}) %all-gather.21.cloned.1.call-update) | async-done | bytes 2097168 | tf_op jit(solution)/shard_map/all_gather | solution.py:70
  706.9 19.0 %psum.67 = f32[128]{0:T(128)S(1)} all-reduce(f32[128]{0:T(128)S(1)} %get-tuple-element.199), channel_id=1, replica_groups=mesh['grid'=8,'band'=4] {'grid'}, use_global_device_ids=true, to_apply=%region_17.20 | all-reduce | flops 128 | bytes 1024 | tf_op jit(solution)/shard_map/psum | solution.py:76
  726.1 17.3 %psum.68 = f32[128]{0:T(128)S(1)} all-reduce(f32[128]{0:T(128)S(1)} %multiply_reduce_fusion.2), channel_id=1, replica_groups=mesh['grid'=8,'band'=4] {'grid'}, use_global_device_ids=true, to_apply=%region_19.22 | all-reduce | flops 128 | bytes 1024 | tf_op jit(solution)/shard_map/psum | solution.py:78
  746.5 21.4 %all-gather.17.cloned.1.call-done = f32[4,16,16,512]{3,2,1,0:T(8,128)} async-done(((f32[4,16,16,128]{3,2,1,0:T(8,128)}), f32[4,16,16,512]{3,2,1,0:T(8,128)}) %all-gather.17.cloned.1.call-update) | async-done | bytes 2097168 | tf_op jit(solution)/shard_map/all_gather | solution.py:62
  775.0 78.2 %all-reduce.9.cloned.1.call-done = f32[512,512]{0,1:T(8,128)} async-done(((f32[512,512]{0,1:T(8,128)}), f32[512,512]{0,1:T(8,128)}) %all-reduce.9.cloned.1.call-update) | async-done | bytes 1048592 | tf_op jit(solution)/shard_map/psum | solution.py:65
  933.4 11.7 %cholesky.575 = f32[128,128]{1,0:T(8,128)S(1)} custom-call(f32[128,128]{1,0:T(8,128)S(1)} %convolution_subtract_fusion.15), custom_call_target="Cholesky" | custom-call | tf_op jit(solution)/shard_map/jit(cholesky)/cholesky | solution.py:66
  952.3 14.2 %while.8 = (s32[]{:T(128)}, f32[512,512]{1,0:T(8,128)}, s32[4,2]{0,1:T(2,128)S(1)}, f32[4,128,128]{2,1,0:T(8,128)}, s32[]{:T(128)}) while((s32[]{:T(128)}, f32[512,512]{1,0:T(8,128)}, s32[4,2]{0,1:T(2,128)S(1)}, f32[4,128,128]{2,1,0:T(8,128)}, s32[]{:T(128)}) %tuple.161), condition=%wide.while_cond.clone.1, body=%wide.while_body.clone.1.sunk | while | flops 2 | bytes 132705 | solution.py:67
  966.5 40.7 %custom-call.42 = f32[4,128,128]{1,2,0:T(8,128)} custom-call(f32[4,128,128]{2,1,0:T(8,128)} %get-tuple-element.27), custom_call_target="InvertDiagBlocksLowerTriangular" | custom-call | tf_op jit(solution)/shard_map/jit(_solve_triangular)/triangular_solve | solution.py:67
  1023.9 20.8 %collective-permute-done.4 = f32[4,16,16,128]{3,2,1,0:T(8,128)} collective-permute-done((f32[4,16,16,128]{3,2,1,0:T(8,128)S(1)}, f32[4,16,16,128]{3,2,1,0:T(8,128)}, u32[]{:S(2)}, u32[]{:S(2)}) %collective-permute-start.4) | collective-permute-done | bytes 524320 | tf_op jit(solution)/shard_map/ppermute | solution.py:22
  1050.9 25.2 %all-gather.23.cloned.1.call-done = f32[4096,128]{0,1:T(8,128)} async-done(((f32[512,128]{0,1:T(8,128)}), f32[4096,128]{0,1:T(8,128)}) %all-gather.23.cloned.1.call-update) | async-done | bytes 2097168 | tf_op jit(solution)/shard_map/all_gather | solution.py:70
  1082.7 19.0 %psum.70 = f32[128]{0:T(128)S(1)} all-reduce(f32[128]{0:T(128)S(1)} %get-tuple-element.203), channel_id=1, replica_groups=mesh['grid'=8,'band'=4] {'grid'}, use_global_device_ids=true, to_apply=%region_23.26 | all-reduce | flops 128 | bytes 1024 | tf_op jit(solution)/shard_map/psum | solution.py:76
  1101.9 17.3 %psum.71 = f32[128]{0:T(128)S(1)} all-reduce(f32[128]{0:T(128)S(1)} %multiply_reduce_fusion), channel_id=1, replica_groups=mesh['grid'=8,'band'=4] {'grid'}, use_global_device_ids=true, to_apply=%region_25.28 | all-reduce | flops 128 | bytes 1024 | tf_op jit(solution)/shard_map/psum | solution.py:78
  (307 shorter events, 336.6 us)
Async XLA Ops:
  7.2 27.9 %all-gather.11.cloned.1.call-start = ((), (), s32[]{:S(2)}) async-start(), calls=%async_computation | async-start | bytes 2621440 | tf_op jit(solution)/shard_map/all_gather | solution.py:62
  7.9 112.4 %all-reduce.5.cloned.1.call-start = ((), (), s32[]{:S(2)}) async-start(), calls=%async_computation.1 | async-start | bytes 2097152 | tf_op jit(solution)/shard_map/psum | solution.py:65
  41.9 225.5 %all-gather.13.cloned.1.call-start = ((), (), s32[]{:S(2)}) async-start(), calls=%async_computation.2 | async-start | bytes 2621440 | tf_op jit(solution)/shard_map/all_gather | solution.py:55
  42.6 281.4 %all-gather.19.cloned.1.call-start = ((), (), s32[]{:S(2)}) async-start(), calls=%async_computation.7 | async-start | bytes 2359296 | tf_op jit(solution)/shard_map/all_gather | solution.py:70
  43.2 216.9 %copy-start.4 = (f32[512,512]{1,0:T(8,128)}, f32[512,512]{1,0:T(8,128)S(1)}, u32[]{:S(2)}) copy-start(f32[512,512]{1,0:T(8,128)S(1)} %fusion.6) | copy-start | bytes 3145732
  120.3 1.7 copy-start.9
  258.8 2.4 copy-start.1
  263.6 27.7 %collective-permute-start = (f32[4,16,16,128]{3,2,1,0:T(8,128)S(1)}, f32[4,16,16,128]{3,2,1,0:T(8,128)S(1)}, u32[]{:S(2)}, u32[]{:S(2)}) collective-permute-start(f32[4,16,16,128]{3,2,1,0:T(8,128)S(1)} %bitcast.268), channel_id=1, source_target_pairs={{4,0},{8,4},{12,8},{16,12},{20,16},{24,20},{28,24},{0,28},{5,1},{9... | collective-permute-start | bytes 1572872 | tf_op jit(solution)/shard_map/ppermute | solution.py:22
  266.6 24.7 %collective-permute-start.1 = (f32[4,16,16,128]{3,2,1,0:T(8,128)S(1)}, f32[4,16,16,128]{3,2,1,0:T(8,128)S(1)}, u32[]{:S(2)}, u32[]{:S(2)}) collective-permute-start(f32[4,16,16,128]{3,2,1,0:T(8,128)S(1)} %bitcast.269), channel_id=1, source_target_pairs={{0,4},{4,8},{8,12},{12,16},{16,20},{20,24},{24,28},{28,0},{1,5},{5... | collective-permute-start | bytes 1572872 | tf_op jit(solution)/shard_map/ppermute | solution.py:19
  270.9 121.3 %all-gather.15.cloned.1.call-start = ((), (), s32[]{:S(2)}) async-start(), calls=%async_computation.3 | async-start | bytes 2621440 | tf_op jit(solution)/shard_map/all_gather | solution.py:62
  272.1 20.1 %copy-start.19 = (f32[4,16,16]{2,1,0:T(8,128)S(1)}, f32[4,16,16]{2,1,0:T(8,128)}, u32[]{:S(2)}) copy-start(f32[4,16,16]{2,1,0:T(8,128)} %param.8) | copy-start | bytes 12292
  272.1 20.1 %copy-start.22 = (f32[4,16,1,128]{3,2,1,0:T(1,128)S(1)}, f32[4,16,1,128]{3,2,1,0:T(1,128)}, u32[]{:S(2)}) copy-start(f32[4,16,1,128]{3,2,1,0:T(1,128)} %get-tuple-element.142) | copy-start | bytes 98308
  324.0 3.8 copy-start.16
  370.8 106.6 %all-reduce.7.cloned.1.call-start = ((), (), s32[]{:S(2)}) async-start(), calls=%async_computation.4 | async-start | bytes 2097152 | tf_op jit(solution)/shard_map/psum | solution.py:65
  399.0 301.2 %all-gather.21.cloned.1.call-start = ((), (), s32[]{:S(2)}) async-start(), calls=%async_computation.8 | async-start | bytes 2359296 | tf_op jit(solution)/shard_map/all_gather | solution.py:70
  477.4 2.7 copy-start.10
  532.4 99.2 %copy-start.5 = (f32[512,512]{1,0:T(8,128)S(1)}, f32[512,512]{1,0:T(8,128)}, u32[]{:S(2)}) copy-start(f32[512,512]{1,0:T(8,128)} %copy-done.4) | copy-start | bytes 3145732
  631.5 5.3 copy-start.21
  634.1 5.2 copy-start.3
  641.2 27.8 %collective-permute-start.2 = (f32[4,16,16,128]{3,2,1,0:T(8,128)S(1)}, f32[4,16,16,128]{3,2,1,0:T(8,128)}, u32[]{:S(2)}, u32[]{:S(2)}) collective-permute-start(f32[4,16,16,128]{3,2,1,0:T(8,128)S(1)} %bitcast.230), channel_id=1, source_target_pairs={{4,0},{8,4},{12,8},{16,12},{20,16},{24,20},{28,24},{0,28},{5,1},{9... | collective-permute-start | bytes 1572872 | tf_op jit(solution)/shard_map/ppermute | solution.py:22
  644.2 24.8 %collective-permute-start.3 = (f32[4,16,16,128]{3,2,1,0:T(8,128)S(1)}, f32[4,16,16,128]{3,2,1,0:T(8,128)}, u32[]{:S(2)}, u32[]{:S(2)}) collective-permute-start(f32[4,16,16,128]{3,2,1,0:T(8,128)S(1)} %bitcast.231), channel_id=1, source_target_pairs={{0,4},{4,8},{8,12},{12,16},{16,20},{20,24},{24,28},{28,0},{1,5},{5... | collective-permute-start | bytes 1572872 | tf_op jit(solution)/shard_map/ppermute | solution.py:19
  647.2 120.7 %all-gather.17.cloned.1.call-start = ((), (), s32[]{:S(2)}) async-start(), calls=%async_computation.5 | async-start | bytes 2621440 | tf_op jit(solution)/shard_map/all_gather | solution.py:62
  648.1 20.9 %copy-start.23 = (f32[4,16,1,128]{3,2,1,0:T(1,128)S(1)}, f32[4,16,1,128]{3,2,1,0:T(1,128)}, u32[]{:S(2)}) copy-start(f32[4,16,1,128]{3,2,1,0:T(1,128)} %get-tuple-element.110) | copy-start | bytes 98308
  746.4 106.7 %all-reduce.9.cloned.1.call-start = ((), (), s32[]{:S(2)}) async-start(), calls=%async_computation.6 | async-start | bytes 2097152 | tf_op jit(solution)/shard_map/psum | solution.py:65
  774.7 301.4 %all-gather.23.cloned.1.call-start = ((), (), s32[]{:S(2)}) async-start(), calls=%async_computation.9 | async-start | bytes 2359296 | tf_op jit(solution)/shard_map/all_gather | solution.py:70
  853.1 2.7 copy-start.11
  908.2 99.0 %copy-start.6 = (f32[512,512]{1,0:T(8,128)S(1)}, f32[512,512]{1,0:T(8,128)}, u32[]{:S(2)}) copy-start(f32[512,512]{1,0:T(8,128)} %copy-done.4) | copy-start | bytes 3145732
  1007.2 5.3 copy-start.20
  1009.8 5.2 copy-start.2
  1016.9 27.8 %collective-permute-start.4 = (f32[4,16,16,128]{3,2,1,0:T(8,128)S(1)}, f32[4,16,16,128]{3,2,1,0:T(8,128)}, u32[]{:S(2)}, u32[]{:S(2)}) collective-permute-start(f32[4,16,16,128]{3,2,1,0:T(8,128)S(1)} %bitcast.249), channel_id=1, source_target_pairs={{4,0},{8,4},{12,8},{16,12},{20,16},{24,20},{28,24},{0,28},{5,1},{9... | collective-permute-start | bytes 1572872 | tf_op jit(solution)/shard_map/ppermute | solution.py:22
  1019.9 24.8 %collective-permute-start.5 = (f32[4,16,16,128]{3,2,1,0:T(8,128)S(1)}, f32[4,16,16,128]{3,2,1,0:T(8,128)}, u32[]{:S(2)}, u32[]{:S(2)}) collective-permute-start(f32[4,16,16,128]{3,2,1,0:T(8,128)S(1)} %bitcast.250), channel_id=1, source_target_pairs={{0,4},{4,8},{8,12},{12,16},{16,20},{20,24},{24,28},{28,0},{1,5},{5... | collective-permute-start | bytes 1572872 | tf_op jit(solution)/shard_map/ppermute | solution.py:19
  1023.7 20.9 %copy-start.24 = (f32[4,16,1,128]{3,2,1,0:T(1,128)S(1)}, f32[4,16,1,128]{3,2,1,0:T(1,128)}, u32[]{:S(2)}) copy-start(f32[4,16,1,128]{3,2,1,0:T(1,128)} %get-tuple-element.78) | copy-start | bytes 98308
  (9 other events, 9.5 us)
Sparse Core Ops, SparseCore 0:
  9.5 25.5 all-gather.10
  42.0 78.3 all-reduce.4
  121.9 22.4 all-gather.12
  271.1 52.8 all-gather.18
  370.9 21.2 all-gather.14
  399.1 78.2 all-reduce.6
  647.3 52.8 all-gather.20
  746.5 21.3 all-gather.16
  774.8 78.2 all-reduce.8
  1023.2 52.8 all-gather.22
